TPU v7x, 512 devices: a whole 4x8x8 slice. The times are simulated.
512 devices in a mesh: blk: 128 (over z, y, core), col: 4 (over x).
Axes of the slice: x: 4, y: 8, z: 8, core: 2. Of those that a mesh axis runs over, the one named last changes fastest.
Arguments:
- kernel: float32 [8192, 4, 2048], P('blk', 'col'), may hold values from -8 to 60
- ritz_block: float32 [8192, 128], P(('blk', 'col')), may hold values from -0.0625 to 0.0625
- search_block: float32 [8192, 128], P(('blk', 'col')), may hold values from -0.0625 to 0.0625
- precond_diag: float32 [8192], P(('blk', 'col')), may hold values from 3 to 30
Outputs:
- new_ritz: float32 [8192, 128], P(('blk', 'col'))
- correction: float32 [8192, 128], P(('blk', 'col'))
- residual_norms: float32 [2, 128], replicated
All inputs are finite; a program needn't handle non-finite values.
Results may differ from a plain program's by a relative error of at most 0.0003.
Values sent between devices are 32-bit elements; how exact they have to be, the bound alone decides.
A program may use at most 64 MiB of HBM per device.

v0:
```python
import jax
import jax.numpy as jnp
from jax import lax
from jax.sharding import Mesh
from jax.sharding import PartitionSpec as P

ITERS = 2
BLK = ("blk_0", "blk_1", "blk_2")
BLK_COL = ("blk_0", "blk_1", "blk_2", "col")


highest = lax.Precision.HIGHEST


def side_by_side(arrays, axis, dim, along):
    both = jnp.concatenate(arrays, axis=along)
    out, at, done = (lax.all_gather(both, axis, axis=dim, tiled=True), 0, [])
    for a in arrays:
        done.append(lax.slice_in_dim(out, at, at + a.shape[along], axis=along))
        at += a.shape[along]
    return tuple(done)


def split_up(value, dim, length):
    before, after = (value.shape[:dim], value.shape[dim + 1 :])
    return jnp.moveaxis(value.reshape(*before, length, -1, *after), dim, 0)


def sum_at_owner(value, axis, dim):
    length = lax.axis_size(axis)
    tiles = lax.all_to_all(split_up(value, dim, length), axis, 0, 0, tiled=True)
    return jnp.sum(tiles, axis=0)


def sent_to_all(value, axis):
    length = lax.axis_size(axis)
    return lax.all_to_all(
        jnp.broadcast_to(value[None], (length, *value.shape)), axis, 0, 0, tiled=True
    )


def joined_along(tiles, dim):
    tiles = jnp.moveaxis(tiles, 0, dim)
    shape = tiles.shape
    return tiles.reshape(*shape[:dim], shape[dim] * shape[dim + 1], *shape[dim + 2 :])


def gather_axes(value, axes, dim):
    far, near = axes
    initial = sent_to_all(value, far)
    tiles = jnp.swapaxes(sent_to_all(initial, near), 0, 1)
    return joined_along(tiles.reshape(-1, *value.shape), dim)


def sum_by_axis(value, axes, dim):
    far, near = axes
    own = sum_at_owner(split_up(value, dim, lax.axis_size(far)), near, dim + 1)
    return jnp.sum(lax.all_to_all(own, far, 0, 0, tiled=True), axis=0)


def filled_up(lines, length):
    spare = -len(lines) % length
    return jnp.pad(lines, [(0, spare)] + [(0, 0)] * (lines.ndim - 1))


def sum_by_parts(value, axes):
    own = sum_by_axis(filled_up(value, lax.axis_size(axes[0]) * lax.axis_size(axes[1])), axes, 0)
    whole = gather_axes(own, axes, 0)
    return whole[: len(value)].reshape(value.shape)


def packed_total(arrays, axis):
    flat, at, done = (jnp.concatenate([a.reshape(-1) for a in arrays]), 0, [])
    total = sum_by_parts(flat, axis)
    for a in arrays:
        done.append(total[at : at + a.size].reshape(a.shape))
        at += a.size
    return tuple(done)


def taken_together(value, axis):
    everything = sent_to_all(value, axis)
    return jnp.sum(everything, axis=0)


def over_axes(value, axes):
    far, near = axes
    return taken_together(taken_together(value, near), far)


def inner(former, latter):
    return lax.dot_general(
        former,
        latter,
        (((0,), (0,)), ((), ())),
        precision=highest,
        preferred_element_type=jnp.float32,
    )


def coefficients(blocks, width):
    ritz_ritz, ritz_search, search_search, ritz_image, ritz_wimage, search_wimage = blocks
    metric = jnp.concatenate(
        [
            jnp.concatenate([ritz_ritz, ritz_search], 1),
            jnp.concatenate([ritz_search.T, search_search], 1),
        ],
        0,
    )
    projected = jnp.concatenate(
        [
            jnp.concatenate([ritz_image, ritz_wimage], 1),
            jnp.concatenate([ritz_wimage.T, search_wimage], 1),
        ],
        0,
    )
    lower_metric = jnp.linalg.cholesky(metric)
    halfway = lax.linalg.triangular_solve(
        lower_metric, projected[:, :width], left_side=True, lower=True
    )
    powered = lax.linalg.triangular_solve(
        lower_metric, halfway, left_side=True, lower=True, transpose_a=True
    )
    hermite = jnp.dot(powered.T, jnp.dot(metric, powered, precision=highest), precision=highest)
    lower_hermite = jnp.linalg.cholesky(hermite)
    mixing = lax.linalg.triangular_solve(
        lower_hermite, powered, left_side=False, lower=True, transpose_a=True
    )
    ritz_values = jnp.dot(
        mixing.T, jnp.dot(projected, mixing, precision=highest), precision=highest
    )
    return (mixing, ritz_values)


def update(vectors, images, search, search_images, mixing, ritz_values, precond):
    width = vectors.shape[1]
    upper_part = mixing[:width]
    lower_part = mixing[width:]
    next_ritz = jnp.dot(vectors, upper_part, precision=highest) + jnp.dot(
        search, lower_part, precision=highest
    )
    next_image = jnp.dot(images, upper_part, precision=highest) + jnp.dot(
        search_images, lower_part, precision=highest
    )
    residual = next_image - jnp.dot(next_ritz, ritz_values, precision=highest)
    squares = jnp.sum(residual * residual, axis=0)
    divisor = jnp.maximum(jnp.abs(precond[:, None] - jnp.diagonal(ritz_values)[None, :]), 1.0)
    return (next_ritz, next_image, residual / divisor, squares)


def per_device(kernel, ritz_block, search_block, precond_diag):
    kernel_rows = kernel[:, 0, :]
    width = ritz_block.shape[1]

    def accumulate(segment):
        return jnp.dot(kernel_rows, segment, precision=highest, preferred_element_type=jnp.float32)

    segments = side_by_side((ritz_block, search_block), BLK, 0, 1)
    part_ritz = accumulate(segments[0])
    part_search = accumulate(segments[1])
    joined = jnp.concatenate([part_ritz, part_search], 1)
    summed = sum_at_owner(joined, "col", 0)
    images = summed[:, :width]
    search_images = summed[:, width:]
    vectors = ritz_block
    search = search_block
    norm_rows = []
    pending = None
    ritz_values = None
    for iteration in range(ITERS):
        if iteration > 0:
            partial_value = accumulate(gather_axes(search, (("blk_0", "blk_1"), "blk_2"), 0))
            search_images = sum_at_owner(partial_value, "col", 0)
        if iteration == 0:
            local_blocks = (
                inner(vectors, vectors),
                inner(vectors, search),
                inner(search, search),
                inner(vectors, images),
                inner(vectors, search_images),
                inner(search, search_images),
            )
            blocks = packed_total(
                (
                    local_blocks[0],
                    local_blocks[1],
                    local_blocks[2],
                    local_blocks[3],
                    local_blocks[4],
                    local_blocks[5],
                ),
                (("blk_0", "blk_1"), ("blk_2", "col")),
            )
        else:
            gathered_sums = packed_total(
                (
                    inner(vectors, search),
                    inner(search, search),
                    inner(vectors, search_images),
                    inner(search, search_images),
                    pending,
                ),
                (("blk_0", "blk_1"), ("blk_2", "col")),
            )
            identity = jnp.eye(width, dtype=jnp.float32)
            blocks = (
                identity,
                gathered_sums[0],
                gathered_sums[1],
                ritz_values,
                gathered_sums[2],
                gathered_sums[3],
            )
            norm_rows.append(jnp.sqrt(gathered_sums[4]))
        mixing, ritz_values = coefficients(blocks, width)
        vectors, images, search, squares = update(
            vectors, images, search, search_images, mixing, ritz_values, precond_diag
        )
        pending = squares
    norm_rows.append(jnp.sqrt(over_axes(pending, (("blk_0", "blk_1"), ("blk_2", "col")))))
    return (vectors, search, jnp.stack(norm_rows, 0))


def solution(mesh):
    torus = Mesh(
        mesh.devices.reshape(8, 8, 2, mesh.shape["col"]), ("blk_0", "blk_1", "blk_2", "col")
    )
    placed = (P(BLK, "col", None), P(BLK_COL, None), P(BLK_COL, None), P(BLK_COL))
    return jax.shard_map(
        per_device,
        mesh=torus,
        in_specs=placed,
        out_specs=(P(BLK_COL, None), P(BLK_COL, None), P()),
        check_vma=False,
    )
```

profile of v0, /device:TPU:1, one launch (start us, length us, event | category | flops | bytes accessed | tf_op | source)
XLA Modules:
  0.0 496.3 jit_solution(5252868300080131623)
XLA Ops:
  7.2 1.4 pad_maximum_fusion.12
  8.6 1.1 fusion.6
  9.7 1.0 fusion.5
  10.7 89.4 %all-gather.2.cloned.1.call-done = f32[2048,256]{1,0:T(8,128)} async-done(((f32[16,256]{1,0:T(8,128)}), f32[2048,256]{1,0:T(8,128)}) %all-gather.2.cloned.1.call-update) | async-done | bytes 2097168 | tf_op jit(solution)/shard_map/all_gather | solution.py:17
  100.1 2.2 convolution_bitcast_fusion.12
  102.4 2.1 convolution_bitcast_fusion.13
  105.2 4.0 all-to-all-start
  109.4 4.2 all-to-all-done
  115.2 13.5 %all_to_all.85 = f32[8,64,192]{2,1,0:T(8,128)S(1)} all-to-all(f32[8,64,192]{2,1,0:T(8,128)S(1)} %copy.99), channel_id=1, replica_groups=mesh['blk_0'=8,'blk_1'=8,'blk_2'=2,'col'=4] {'blk_2','col'}, dimensions={0} | all-to-all | bytes 786432 | tf_op jit(solution)/shard_map/all_to_all | solution.py:31
  128.7 19.5 %all_to_all.86 = f32[64,1,192]{2,1,0:T(1,128)S(1)} all-to-all(f32[64,1,192]{2,1,0:T(1,128)S(1)} %all_to_all.54), channel_id=1, replica_groups=mesh['blk_0'=8,'blk_1'=8,'blk_2'=2,'col'=4] {'blk_0','blk_1'}, dimensions={0} | all-to-all | bytes 98304 | tf_op jit(solution)/shard_map/all_to_all | solution.py:58
  148.3 14.9 %all_to_all.82 = f32[64,1,192]{2,1,0:T(1,128)S(1)} all-to-all(f32[64,1,192]{2,1,0:T(1,128)S(1)} %broadcast_in_dim.28), channel_id=1, replica_groups=mesh['blk_0'=8,'blk_1'=8,'blk_2'=2,'col'=4] {'blk_0','blk_1'}, dimensions={0} | all-to-all | bytes 98304 | tf_op jit(solution)/shard_map/all_to_all | solution.py:37
  164.1 6.6 %all-to-all-start.4 = ((f32[8,64,192]{2,1,0:T(8,128)}), f32[8,64,192]{2,1,0:T(8,128)S(1)}, u32[]{:S(2)}, u32[]{:S(2)}) async-start(f32[8,64,192]{2,1,0:T(8,128)} %broadcast_in_dim.30), calls=%async_computation.4 | async-start | bytes 1048576 | tf_op jit(solution)/shard_map/all_to_all | solution.py:37
  170.7 9.3 %all-to-all-done.4 = f32[8,64,192]{2,1,0:T(8,128)S(1)} async-done(((f32[8,64,192]{2,1,0:T(8,128)}), f32[8,64,192]{2,1,0:T(8,128)S(1)}, u32[]{:S(2)}, u32[]{:S(2)}) %all-to-all-start.4) | async-done | bytes 393248 | tf_op jit(solution)/shard_map/all_to_all | solution.py:37
  181.0 11.7 %cholesky.172 = f32[128,128]{1,0:T(8,128)S(1)} custom-call(f32[128,128]{1,0:T(8,128)S(1)} %cholesky.258), custom_call_target="Cholesky" | custom-call | tf_op jit(solution)/shard_map/jit(cholesky)/cholesky | solution.py:117
  192.8 9.8 %custom-call.27 = f32[1,128,128]{1,2,0:T(8,128)S(1)} custom-call(f32[1,128,128]{2,1,0:T(8,128)S(1)} %get-tuple-element.80), custom_call_target="InvertDiagBlocksLowerTriangular" | custom-call | tf_op jit(solution)/shard_map/jit(cholesky)/cholesky | solution.py:117
  203.1 11.7 %cholesky.189 = f32[128,128]{1,0:T(8,128)S(1)} custom-call(f32[128,128]{1,0:T(8,128)S(1)} %convolution_subtract_fusion.5), custom_call_target="Cholesky" | custom-call | tf_op jit(solution)/shard_map/jit(cholesky)/cholesky | solution.py:117
  217.1 4.1 while.8
  217.7 1.4 bitcast_dynamic-update-slice_fusion.7
  219.7 1.4 bitcast_dynamic-update-slice_fusion.7
  221.2 20.1 %custom-call.29 = f32[2,128,128]{1,2,0:T(8,128)S(1)} custom-call(f32[2,128,128]{2,1,0:T(8,128)S(1)} %get-tuple-element.37), custom_call_target="InvertDiagBlocksLowerTriangular" | custom-call | tf_op jit(solution)/shard_map/triangular_solve/custom-call.5 | solution.py:121
  244.2 11.7 %cholesky.204 = f32[128,128]{1,0:T(8,128)S(1)} custom-call(f32[128,128]{1,0:T(8,128)S(1)} %fusion.48), custom_call_target="Cholesky" | custom-call | tf_op jit(solution)/shard_map/jit(cholesky)/cholesky | solution.py:125
  257.3 9.8 %custom-call.30 = f32[1,128,128]{1,2,0:T(8,128)S(1)} custom-call(f32[1,128,128]{2,1,0:T(8,128)S(1)} %fusion.36), custom_call_target="InvertDiagBlocksLowerTriangular" | custom-call | tf_op jit(solution)/shard_map/triangular_solve/custom-call.6 | solution.py:126
  269.0 1.3 gather_fusion
  271.4 4.6 all-to-all-start.5
  276.4 17.7 %all-to-all-done.5 = f32[64,16,128]{2,1,0:T(8,128)S(1)} async-done(((f32[64,16,128]{2,1,0:T(8,128)}), f32[64,16,128]{2,1,0:T(8,128)S(1)}, u32[]{:S(2)}, u32[]{:S(2)}) %all-to-all-start.5) | async-done | bytes 524320 | tf_op jit(solution)/shard_map/all_to_all | solution.py:37
  294.1 5.6 %all_to_all.83 = f32[2,64,16,128]{3,2,1,0:T(8,128)S(1)} all-to-all(f32[2,64,16,128]{3,2,1,0:T(8,128)S(1)} %broadcast_in_dim.32), channel_id=1, replica_groups=mesh['blk_0'=8,'blk_1'=8,'blk_2'=2,'col'=4] {'blk_2'}, dimensions={0} | all-to-all | bytes 2097152 | tf_op jit(solution)/shard_map/all_to_all | solution.py:37
  299.9 1.5 fusion.9
  301.4 3.4 all-to-all-start.7
  305.1 4.0 all-to-all-done.7
  310.5 13.6 %all_to_all.87 = f32[8,64,129]{2,1,0:T(8,128)S(1)} all-to-all(f32[8,64,129]{2,1,0:T(8,128)S(1)} %copy.109), channel_id=1, replica_groups=mesh['blk_0'=8,'blk_1'=8,'blk_2'=2,'col'=4] {'blk_2','col'}, dimensions={0} | all-to-all | bytes 528384 | tf_op jit(solution)/shard_map/all_to_all | solution.py:31
  324.1 16.4 %all_to_all.88 = f32[64,1,129]{2,1,0:T(1,128)S(1)} all-to-all(f32[64,1,129]{2,1,0:T(1,128)S(1)} %all_to_all.62), channel_id=1, replica_groups=mesh['blk_0'=8,'blk_1'=8,'blk_2'=2,'col'=4] {'blk_0','blk_1'}, dimensions={0} | all-to-all | bytes 66048 | tf_op jit(solution)/shard_map/all_to_all | solution.py:58
  340.7 14.9 %all_to_all.84 = f32[64,1,129]{2,1,0:T(1,128)S(1)} all-to-all(f32[64,1,129]{2,1,0:T(1,128)S(1)} %broadcast_in_dim.33), channel_id=1, replica_groups=mesh['blk_0'=8,'blk_1'=8,'blk_2'=2,'col'=4] {'blk_0','blk_1'}, dimensions={0} | all-to-all | bytes 66048 | tf_op jit(solution)/shard_map/all_to_all | solution.py:37
  356.4 6.6 %all-to-all-start.11 = ((f32[8,64,129]{2,1,0:T(8,128)}), f32[8,64,129]{2,1,0:T(8,128)S(1)}, u32[]{:S(2)}, u32[]{:S(2)}) async-start(f32[8,64,129]{2,1,0:T(8,128)} %broadcast_in_dim.35), calls=%async_computation.11 | async-start | bytes 1048576 | tf_op jit(solution)/shard_map/all_to_all | solution.py:37
  363.0 9.3 %all-to-all-done.11 = f32[8,64,129]{2,1,0:T(8,128)S(1)} async-done(((f32[8,64,129]{2,1,0:T(8,128)}), f32[8,64,129]{2,1,0:T(8,128)S(1)}, u32[]{:S(2)}, u32[]{:S(2)}) %all-to-all-start.11) | async-done | bytes 264224 | tf_op jit(solution)/shard_map/all_to_all | solution.py:37
  373.5 11.7 %cholesky.217 = f32[128,128]{1,0:T(8,128)S(1)} custom-call(f32[128,128]{1,0:T(8,128)S(1)} %cholesky.261), custom_call_target="Cholesky" | custom-call | tf_op jit(solution)/shard_map/jit(cholesky)/cholesky | solution.py:117
  385.3 9.8 %custom-call.31 = f32[1,128,128]{1,2,0:T(8,128)S(1)} custom-call(f32[1,128,128]{2,1,0:T(8,128)S(1)} %get-tuple-element.76), custom_call_target="InvertDiagBlocksLowerTriangular" | custom-call | tf_op jit(solution)/shard_map/jit(cholesky)/cholesky | solution.py:117
  395.6 11.7 %cholesky.234 = f32[128,128]{1,0:T(8,128)S(1)} custom-call(f32[128,128]{1,0:T(8,128)S(1)} %convolution_subtract_fusion.2), custom_call_target="Cholesky" | custom-call | tf_op jit(solution)/shard_map/jit(cholesky)/cholesky | solution.py:117
  409.9 4.0 while.9
  410.6 1.4 bitcast_dynamic-update-slice_fusion.8
  412.6 1.4 bitcast_dynamic-update-slice_fusion.8
  414.0 19.9 %custom-call.33 = f32[2,128,128]{1,2,0:T(8,128)S(1)} custom-call(f32[2,128,128]{2,1,0:T(8,128)S(1)} %get-tuple-element.39), custom_call_target="InvertDiagBlocksLowerTriangular" | custom-call | tf_op jit(solution)/shard_map/triangular_solve/custom-call.5 | solution.py:121
  436.6 11.7 %cholesky.249 = f32[128,128]{1,0:T(8,128)S(1)} custom-call(f32[128,128]{1,0:T(8,128)S(1)} %fusion.45), custom_call_target="Cholesky" | custom-call | tf_op jit(solution)/shard_map/jit(cholesky)/cholesky | solution.py:125
  449.6 9.8 %custom-call.34 = f32[1,128,128]{1,2,0:T(8,128)S(1)} custom-call(f32[1,128,128]{2,1,0:T(8,128)S(1)} %fusion.37), custom_call_target="InvertDiagBlocksLowerTriangular" | custom-call | tf_op jit(solution)/shard_map/triangular_solve/custom-call.6 | solution.py:126
  461.5 1.2 gather_fusion.1
  464.3 3.6 all-to-all-start.12
  468.3 4.2 all-to-all-done.12
  473.1 4.6 all-to-all-start.13
  477.8 10.9 %all-to-all-done.13 = f32[64,1,128]{2,1,0:T(1,128)S(1)} async-done(((f32[64,1,128]{2,1,0:T(1,128)}), f32[64,1,128]{2,1,0:T(1,128)S(1)}, u32[]{:S(2)}, u32[]{:S(2)}) %all-to-all-start.13) | async-done | bytes 32800 | tf_op jit(solution)/shard_map/all_to_all | solution.py:37
  (155 shorter events, 30.9 us)
Async XLA Ops:
  7.2 106.4 %copy-start.1 = (f32[16,128]{1,0:T(8,128)S(1)}, f32[16,128]{1,0:T(8,128)}, u32[]{:S(2)}) copy-start(f32[16,128]{1,0:T(8,128)} %param.13) | copy-start | bytes 24580
  7.2 102.0 %copy-start.2 = (f32[16,128]{1,0:T(8,128)S(1)}, f32[16,128]{1,0:T(8,128)}, u32[]{:S(2)}) copy-start(f32[16,128]{1,0:T(8,128)} %param.14) | copy-start | bytes 24580
  7.2 95.2 %copy-start = (f32[64,1,2048]{2,1,0:T(1,128)S(1)}, f32[64,1,2048]{2,1,0:T(1,128)}, u32[]{:S(2)}) copy-start(f32[64,1,2048]{2,1,0:T(1,128)} %param.12) | copy-start | bytes 1572868
  7.2 92.9 %all-gather.2.cloned.1.call-start = ((), (), s32[]{:S(2)}) async-start(), calls=%async_computation.14 | async-start | bytes 2113536 | tf_op jit(solution)/shard_map/all_gather | solution.py:17
  105.2 8.4 %all-to-all-start = ((f32[4,16,256]{2,1,0:T(8,128)}), f32[4,16,256]{2,1,0:T(8,128)S(1)}, u32[]{:S(2)}, u32[]{:S(2)}) async-start(f32[4,16,256]{2,1,0:T(8,128)} %bitcast.5), calls=%async_computation | async-start | bytes 131072 | tf_op jit(solution)/shard_map/all_to_all | solution.py:31
  164.1 15.9 %all-to-all-start.4 = ((f32[8,64,192]{2,1,0:T(8,128)}), f32[8,64,192]{2,1,0:T(8,128)S(1)}, u32[]{:S(2)}, u32[]{:S(2)}) async-start(f32[8,64,192]{2,1,0:T(8,128)} %broadcast_in_dim.30), calls=%async_computation.4 | async-start | bytes 1048576 | tf_op jit(solution)/shard_map/all_to_all | solution.py:37
  242.4 28.0 %copy-start.4 = (f32[16]{0:T(128)S(1)}, f32[16]{0:T(128)}, u32[]{:S(2)}) copy-start(f32[16]{0:T(128)} %param.15) | copy-start | bytes 196
  271.4 22.7 %all-to-all-start.5 = ((f32[64,16,128]{2,1,0:T(8,128)}), f32[64,16,128]{2,1,0:T(8,128)S(1)}, u32[]{:S(2)}, u32[]{:S(2)}) async-start(f32[64,16,128]{2,1,0:T(8,128)} %broadcast_in_dim.31), calls=%async_computation.5 | async-start | bytes 1048576 | tf_op jit(solution)/shard_map/all_to_all | solution.py:37
  301.4 7.7 %all-to-all-start.7 = ((f32[4,16,128]{2,1,0:T(8,128)}), f32[4,16,128]{2,1,0:T(8,128)S(1)}, u32[]{:S(2)}, u32[]{:S(2)}) async-start(f32[4,16,128]{2,1,0:T(8,128)} %bitcast.33), calls=%async_computation.7 | async-start | bytes 65536 | tf_op jit(solution)/shard_map/all_to_all | solution.py:31
  356.4 15.9 %all-to-all-start.11 = ((f32[8,64,129]{2,1,0:T(8,128)}), f32[8,64,129]{2,1,0:T(8,128)S(1)}, u32[]{:S(2)}, u32[]{:S(2)}) async-start(f32[8,64,129]{2,1,0:T(8,128)} %broadcast_in_dim.35), calls=%async_computation.11 | async-start | bytes 1048576 | tf_op jit(solution)/shard_map/all_to_all | solution.py:37
  462.9 26.3 %copy-start.3 = (f32[16,128]{1,0:T(8,128)}, f32[16,128]{1,0:T(8,128)S(1)}, u32[]{:S(2)}) copy-start(f32[16,128]{1,0:T(8,128)S(1)} %convolution_add_fusion.1) | copy-start | bytes 24580
  464.3 8.1 %all-to-all-start.12 = ((f32[8,1,128]{2,1,0:T(1,128)}), f32[8,1,128]{2,1,0:T(1,128)S(1)}, u32[]{:S(2)}, u32[]{:S(2)}) async-start(f32[8,1,128]{2,1,0:T(1,128)} %broadcast_in_dim.36), calls=%async_computation.12 | async-start | bytes 8192 | tf_op jit(solution)/shard_map/all_to_all | solution.py:37
  473.1 15.5 %all-to-all-start.13 = ((f32[64,1,128]{2,1,0:T(1,128)}), f32[64,1,128]{2,1,0:T(1,128)S(1)}, u32[]{:S(2)}, u32[]{:S(2)}) async-start(f32[64,1,128]{2,1,0:T(1,128)} %broadcast_in_dim.37), calls=%async_computation.13 | async-start | bytes 65536 | tf_op jit(solution)/shard_map/all_to_all | solution.py:37
Sparse Core Ops, SparseCore 0:
  11.1 88.9 all-gather.1
where the time goes:
time: 502 us; the launch traced here: 496 us
  other arithmetic  157 us (31%)
  waiting for transfers between devices  149 us (30%)
  blocking collectives  98.3 us (20%)
  starting transfers between devices  33.3 us (7%)
  matrix products  21.1 us (4%)
  local copies, waits for them, and re-layouts  19.3 us (4%)
  between operations  17.8 us (4%)
    all_gather x1, waiting for transfers between devices, side_by_side(): out, at, done = (lax.all_gather(both, axis, axis=dim, tiled=True), 0, [])  89.4 us
    another operation x13, other arithmetic, coefficients(): lower_metric = jnp.linalg.cholesky(metric)  68.6 us
    all_to_all x5, waiting for transfers between devices, sent_to_all(): lax.all_to_all(jnp.broadcast_to(value[None], (length, *value.shape)), axi...  51.4 us
    another operation x5, other arithmetic, coefficients(): lax.linalg.triangular_solve(lower_metric, halfway, left_side=True, lower=...  40 us
    all_to_all x2, blocking collectives, sum_by_axis(): return jnp.sum(lax.all_to_all(own, far, 0, 0, tiled=True), axis=0)  35.9 us
    all_to_all x3, blocking collectives, sent_to_all(): lax.all_to_all(jnp.broadcast_to(value[None], (length, *value.shape)), axi...  35.4 us
    all_to_all x2, blocking collectives, sum_at_owner(): tiles = lax.all_to_all(split_up(value, dim, length), axis, 0, 0, tiled=True)  27 us
    all_to_all x5, starting transfers between devices, sent_to_all(): lax.all_to_all(jnp.broadcast_to(value[None], (length, *value.shape)), axi...  25.9 us
  transfers between devices with their start and end apart: 8, of which 8 were waited for; matrix products, arithmetic and copies ran while one was open for 1% of the time, Pallas kernels for 0%

commit v1 on v0

v1 whole, which is shorter than its diff:
```python
import functools

import jax
import jax.numpy as jnp
from jax import lax
from jax.experimental import pallas as pl
from jax.experimental.pallas import tpu as pltpu
from jax.sharding import Mesh
from jax.sharding import PartitionSpec as P

MESH = pl.DeviceIdType.MESH
BLK = ("blk_0", "blk_1", "blk_2")
BLK_COL = ("blk_0", "blk_1", "blk_2", "col")
V = 128
Q = 16
PANEL = 16
f32 = jnp.float32
bf16 = jnp.bfloat16
highest = lax.Precision.HIGHEST


def dot(a, b, ca=1, cb=0):
    return lax.dot_general(
        a, b, (((ca,), (cb,)), ((), ())), precision=highest, preferred_element_type=f32
    )


def split(a):
    high = a.astype(bf16)
    return high, (a - high.astype(f32)).astype(bf16)


def dot3(a, b, ca=1, cb=0):
    dims = (((ca,), (cb,)), ((), ()))

    def one(x, y):
        return lax.dot_general(x, y, dims, preferred_element_type=f32)

    return one(a[0], b[0]) + (one(a[0], b[1]) + one(a[1], b[0]))


def inverse_factor(matrix, work):
    row = lax.broadcasted_iota(jnp.int32, (V, V), 0)
    lane = lax.broadcasted_iota(jnp.int32, (V, V), 1)
    work[:, :V] = matrix
    work[:, V:] = jnp.where(row == lane, 1.0, 0.0).astype(f32)
    sub = lax.broadcasted_iota(jnp.int32, (PANEL, V), 0)
    for start in range(0, V, PANEL):
        end = start + PANEL
        left = work[start:end, :V]
        right = work[start:end, V:]
        columns = [
            jnp.broadcast_to(left[:, start + t : start + t + 1], (PANEL, V)) for t in range(PANEL)
        ]
        scale = jnp.zeros((PANEL, V), f32)
        for r in range(PANEL):
            inverse = lax.rsqrt(jnp.broadcast_to(columns[r][r : r + 1, :], (PANEL, V)))
            scale = jnp.where(sub == r, inverse, scale)
            if r == PANEL - 1:
                break
            factor = jnp.where(sub > r, columns[r] * inverse, 0.0)
            for t in range(r + 1, PANEL):
                columns[t] = columns[t] - factor * factor[t : t + 1, :]
            factor = factor * inverse
            left = left - factor * left[r : r + 1, :]
            right = right - factor * right[r : r + 1, :]
        left = left * scale
        right = right * scale
        work[start:end, V:] = right
        if end < V:
            lower = dot(left, jnp.concatenate([left, right], 1), 0, 0)
            work[end:, :] = work[end:, :] - lower[end:, :]
    return work[:, V:]


def mixing_of(blocks, work, first):
    ritz_ritz, ritz_search, search_search, ritz_image, cross_image, search_image = blocks
    if first:
        top = inverse_factor(ritz_ritz, work)
        side = dot(top, ritz_search)
    else:
        side = ritz_search
    low = inverse_factor(search_search - dot(side, side, 0, 0), work)
    upper = dot(top, ritz_image) if first else ritz_image
    lower = dot(low, cross_image - dot(side, upper, 0, 0), 1, 0)
    back = inverse_factor(dot(upper, upper, 0, 0) + dot(lower, lower, 0, 0), work)
    upper = dot(upper, back, 1, 1)
    lower = dot(lower, back, 1, 1)
    lower = dot(low, lower, 0, 0)
    upper = upper - dot(side, lower)
    if first:
        upper = dot(top, upper, 0, 0)
    return upper, lower


def coefficients_kernel(first, *refs):
    *ins, mix_ref, ritz_ref, work = refs
    if first:
        metric, projected = ins
        xx, xw, ww = (metric[i * V : (i + 1) * V, :] for i in range(3))
        gxx, gxw, gww = (projected[i * V : (i + 1) * V, :] for i in range(3))
    else:
        sums, last, ritz = ins
        xx = None
        xw, ww, gxw = (sums[i * V : (i + 1) * V, :] for i in range(3))
        gww = last[...]
        gxx = ritz[...]
    upper, lower = mixing_of((xx, xw, ww, gxx, gxw.T, gww), work, first)
    mix_ref[:V, :] = upper
    mix_ref[V:, :] = lower
    one = dot(gxx, upper) + dot(gxw, lower)
    two = dot(gxw, upper, 0, 0) + dot(gww, lower)
    ritz_ref[...] = dot(upper, one, 0, 0) + dot(lower, two, 0, 0)


def coefficients(first, *operands):
    return pl.pallas_call(
        functools.partial(coefficients_kernel, first),
        out_shape=(
            jax.ShapeDtypeStruct((2 * V, V), f32),
            jax.ShapeDtypeStruct((V, V), f32),
        ),
        in_specs=[pl.BlockSpec(memory_space=pltpu.VMEM)] * len(operands),
        out_specs=(pl.BlockSpec(memory_space=pltpu.VMEM),) * 2,
        scratch_shapes=[pltpu.VMEM((V, 2 * V), f32)],
    )(*operands)


class Place:
    def __init__(self, dims):
        self.dims = dims
        self.z, self.y, self.core, self.x = (lax.axis_index(a) for a in BLK_COL)

    def plane(self, axis, step):
        name = ("blk_0", "blk_1")[axis]
        size = self.dims[axis]
        here = (self.z, self.y)[axis]
        return {name: lax.rem(here + step + size, size)}

    def near(self, index):
        dx, dc = index // 2, index % 2
        x = lax.rem(self.x + dx, self.dims[3])
        core = lax.rem(self.core + dc, 2)
        return x, core, {"col": x, "blk_2": core}

    def group(self):
        return self.x * 2 + self.core

    def enter(self, plane):
        barrier = pltpu.get_barrier_semaphore()
        count = 0
        peers = [self.near(i)[2] for i in range(1, 2 * self.dims[3])]
        if plane:
            for axis in range(2):
                peers += [self.plane(axis, s) for s in range(1, self.dims[axis])]
        for peer in peers:
            pl.semaphore_signal(barrier, inc=1, device_id=peer, device_id_type=MESH)
            count += 1
        return barrier, count


def remote(src, dst, send, recv, to):
    return pltpu.make_async_remote_copy(
        src_ref=src,
        dst_ref=dst,
        send_sem=send,
        recv_sem=recv,
        device_id=to,
        device_id_type=MESH,
    )


class Flow:
    def __init__(self, place, buffer, rows, first, sems):
        self.place, self.buffer, self.rows, self.first = place, buffer, rows, first
        self.second = 1 - first
        self.sems = sems
        self.at = 0
        self.sent = []

    def sem(self):
        self.at += 1
        return self.sems.at[0, self.at - 1], self.sems.at[1, self.at - 1]

    def view(self, z, y):
        return self.buffer.at[z, y, self.rows]

    def begin(self):
        p = self.place
        self.own = []
        for step in range(1, p.dims[self.first]):
            ref = self.view(p.z, p.y)
            copy = remote(ref, ref, *self.sem(), p.plane(self.first, step))
            copy.start()
            self.own.append(copy)

    def middle(self):
        for copy in self.own:
            copy.wait_recv()
        self.sent += self.own
        self.moving = {}
        for chunk in range(2):
            for way in (1, -1):
                self.forward(way, chunk, 0)

    def line(self, origin, chunk):
        half = self.place.dims[self.first] // 2
        part = pl.ds(chunk * half, half)
        if self.first == 0:
            return self.buffer.at[part, origin, self.rows]
        return self.buffer.at[origin, part, self.rows]

    def last(self, way, chunk, hop):
        return hop == self.place.dims[self.second] // 2 - 1 and (way == 1) != (chunk == 0)

    def forward(self, way, chunk, hop):
        p = self.place
        size = p.dims[self.second]
        if hop >= size // 2 or self.last(way, chunk, hop):
            return
        here = (p.z, p.y)[self.second]
        ref = self.line(lax.rem(here - way * hop + size, size), chunk)
        copy = remote(ref, ref, *self.sem(), p.plane(self.second, way))
        copy.start()
        self.moving[way, chunk, hop] = copy

    def relay(self, hop):
        for chunk in range(2):
            for way in (1, -1):
                copy = self.moving.get((way, chunk, hop))
                if copy is not None:
                    copy.wait_recv()
                    self.sent.append(copy)
                    self.forward(way, chunk, hop + 1)

    @staticmethod
    def finish(flows):
        for flow in flows:
            flow.middle()
        for hop in range(max(f.place.dims[f.second] // 2 for f in flows)):
            for flow in flows:
                flow.relay(hop)

    @staticmethod
    def drain(flows):
        for flow in flows:
            for copy in flow.sent:
                copy.wait_send()


def flow_sems():
    return pltpu.SemaphoreType.DMA((2, 24))


class Spread:
    def __init__(self, place, source, target, sems):
        self.place = place
        self.copies = []
        for i in range(1, 2 * place.dims[3]):
            x, core, to = place.near(i)
            self.copies.append(
                remote(source(x, core), target(i), sems.at[0, i], sems.at[1, i], to)
            )
        for copy in self.copies:
            copy.start()

    def arrive(self):
        for copy in self.copies:
            copy.wait_recv()

    def drain(self):
        for copy in self.copies:
            copy.wait_send()


class Sum:
    def __init__(self, place, value, pieces, landed, whole, sems):
        self.place, self.pieces, self.landed, self.whole = place, pieces, landed, whole
        self.sems = sems
        pieces[...] = value.reshape(pieces.shape)
        self.scatter = Spread(
            place, lambda x, core: pieces.at[x * 2 + core], lambda i: landed.at[i], sems.at[0]
        )

    def middle(self):
        place, own = self.place, self.place.group()
        self.scatter.arrive()
        total = self.pieces[own]
        for i in range(1, 2 * place.dims[3]):
            total = total + self.landed[i]
        self.whole[own] = total
        self.share = Spread(
            place,
            lambda x, core: self.whole.at[own],
            lambda i: self.whole.at[own],
            self.sems.at[1],
        )

    def arrive(self):
        self.share.arrive()

    def drain(self):
        self.scatter.drain()
        self.share.drain()


def near_sems(*lead):
    return pltpu.SemaphoreType.DMA((*lead, 2, 8))


def sum_scratch(group, rows):
    return [pltpu.VMEM((group, rows, V), f32)] * 3 + [near_sems(2)]


def rows_of(buffer):
    return buffer[...].reshape(-1, buffer.shape[-1])


def images_kernel(
    dims, k_in, x_in, w_in, d_in, metric, projected, yx, yw, zx, zw, kern, diag,
    gx, gw, hx, hw, gd, kraw, kown, kland, part, landed,
    m0, m1, m2, msem, p0, p1, p2, psem,
    load, ksem, sx, sw, tx, tw, sd, rs,
):
    place = Place(dims)
    nz, ny, _, nx = dims
    group = 2 * nx
    barrier, count = place.enter(True)
    loads = [
        pltpu.make_async_copy(x_in, gx.at[place.z, place.y], load.at[0]),
        pltpu.make_async_copy(w_in, gw.at[place.z, place.y], load.at[1]),
        pltpu.make_async_copy(d_in, gd.at[place.z, place.y], load.at[2]),
        pltpu.make_async_copy(k_in, kraw, load.at[3]),
    ]
    for copy in loads:
        copy.start()
    for copy in loads[:3]:
        copy.wait()
    pl.semaphore_wait(barrier, count)
    flows = [
        Flow(place, gx, slice(None), 1, sx),
        Flow(place, gw, slice(None), 0, sw),
    ]
    for flow in flows:
        flow.begin()
    small = Flow(place, gd, slice(None), 1, sd)
    small.begin()
    loads[3].wait()
    i = lax.broadcasted_iota(jnp.int32, (2 * V, 2 * V), 0)
    j = lax.broadcasted_iota(jnp.int32, (2 * V, 2 * V), 1)
    to = ((i // Q) % 2) * V + (i // (2 * Q)) * Q + i % Q
    mover = jnp.where(j == to, 1.0, 0.0).astype(f32)
    for tile in range(kraw.shape[1] // (2 * V)):
        moved = dot(kraw[:, tile * 2 * V : (tile + 1) * 2 * V], mover)
        kown[0, :, tile * V : (tile + 1) * V] = moved[:, :V]
        kown[1, :, tile * V : (tile + 1) * V] = moved[:, V:]
    swap = remote(kown.at[1 - place.core], kland, ksem.at[0], ksem.at[1], place.near(1)[2])
    swap.start()
    Flow.finish(flows + [small])
    swap.wait()
    mine, other = kown[place.core], kland[...]
    kern[0] = mine
    kern[1] = other
    both = split(jnp.concatenate([mine, other], 0))
    y = jnp.concatenate([rows_of(gx), rows_of(gw)], 1)
    ys = split(y)
    image = dot3(both, ys)
    rows = mine.shape[0]
    part[place.core] = image[:rows].reshape(nx, Q, 2 * V)
    part[1 - place.core] = image[rows:].reshape(nx, Q, 2 * V)
    scatter = Spread(place, lambda x, core: part.at[core, x], lambda i: landed.at[i], rs)
    gram = dot3(ys, ys, 0, 0)
    gram = jnp.concatenate([gram[:V, :V], gram[:V, V:], gram[V:, V:]], 0)
    sums = Sum(place, gram, m0, m1, m2, msem)
    scatter.arrive()
    total = part[place.core, place.x]
    for i in range(1, group):
        total = total + landed[i]
    hx[place.z, place.y] = total[:, :V]
    hw[place.z, place.y] = total[:, V:]
    again = [
        Flow(place, hx, slice(None), 1, tx),
        Flow(place, hw, slice(None), 0, tw),
    ]
    for flow in again:
        flow.begin()
    height = nz * ny * Q
    r = lax.broadcasted_iota(jnp.int32, (height, nz * ny), 0)
    b = lax.broadcasted_iota(jnp.int32, (height, nz * ny), 1)
    pick = jnp.where(r // Q == b, 1.0, 0.0).astype(f32)
    entries = dot(pick, gd[...].reshape(nz * ny, V))
    r = lax.broadcasted_iota(jnp.int32, (height, V), 0)
    b = lax.broadcasted_iota(jnp.int32, (height, V), 1)
    entries = jnp.where(r % Q == b, entries, 0.0)
    diag[...] = dot(entries, jnp.ones((V, V), f32))
    yx[...] = y[:, :V]
    yw[...] = y[:, V:]
    sums.middle()
    Flow.finish(again)
    sums.arrive()
    metric[...] = rows_of(m2)
    z = jnp.concatenate([rows_of(hx), rows_of(hw)], 1)
    zx[...] = z[:, :V]
    zw[...] = z[:, V:]
    gram = dot3(ys, split(z), 0, 0)
    gram = jnp.concatenate([gram[:V, :V], gram[:V, V:], gram[V:, V:]], 0)
    more = Sum(place, gram, p0, p1, p2, psem)
    more.middle()
    more.arrive()
    projected[...] = rows_of(p2)
    Flow.drain(flows + [small] + again)
    scatter.drain()
    sums.drain()
    more.drain()


def moved_on(x, w, kx, kw, mix, ritz, diag, norm_only=False):
    eye = jnp.where(
        lax.broadcasted_iota(jnp.int32, (V, V), 0) == lax.broadcasted_iota(jnp.int32, (V, V), 1),
        ritz,
        0.0,
    )
    values = jnp.sum(eye, axis=0, keepdims=True)
    upper, lower = split(mix[:V]), split(mix[V:])
    vectors = dot3(split(x), upper) + dot3(split(w), lower)
    images = dot3(split(kx), upper) + dot3(split(kw), lower)
    residual = images - dot3(split(vectors), split(ritz))
    squares = jnp.sum(residual * residual, axis=0, keepdims=True)
    search = residual / jnp.maximum(jnp.abs(diag - values), 1.0)
    return vectors, images, search, squares


def search_kernel(
    dims, yx, yw, zx, zw, kern, diag, mix, ritz, sums_out, last_out, norm, nx_out, nk_out, nw_out, hk_out,
    part, landed, hk, q0, q1, q2, qsem, l0, l1, l2, lsem, nsum, nland,
    tx, tw, rs, ns,
):
    place = Place(dims)
    group = 2 * dims[3]
    barrier, count = place.enter(True)
    vectors, images, search, squares = moved_on(
        yx[...], yw[...], zx[...], zw[...], mix[...], ritz[...], diag[...]
    )
    ws = split(search)
    rows = kern.shape[1]
    image = dot3(split(kern[...].reshape(2 * rows, -1)), ws)
    part[place.core] = image[:rows].reshape(dims[3], Q, V)
    part[1 - place.core] = image[rows:].reshape(dims[3], Q, V)
    nsum[...] = jnp.broadcast_to(squares, (8, V))
    pl.semaphore_wait(barrier, count)
    scatter = Spread(place, lambda x, core: part.at[core, x], lambda i: landed.at[i], rs)
    left = jnp.concatenate([vectors, search, images], 1)
    sums = Sum(place, dot3(split(left), ws, 0, 0), q0, q1, q2, qsem)
    norms = Spread(place, lambda x, core: nsum, lambda i: nland.at[i], ns)
    scatter.arrive()
    total = part[place.core, place.x]
    for i in range(1, group):
        total = total + landed[i]
    hk[place.z, place.y] = total
    flows = [
        Flow(place, hk, slice(0, Q // 2), 1, tx),
        Flow(place, hk, slice(Q // 2, Q), 0, tw),
    ]
    for flow in flows:
        flow.begin()
    nx_out[...] = vectors
    nk_out[...] = images
    nw_out[...] = search
    sums.middle()
    Flow.finish(flows)
    sums.arrive()
    sums_out[...] = rows_of(q2)
    norms.arrive()
    squares = nsum[...]
    for i in range(1, group):
        squares = squares + nland[i]
    norm[...] = jnp.sqrt(squares)
    final = rows_of(hk)
    hk_out[...] = final
    more = Sum(place, dot3(ws, split(final), 0, 0), l0, l1, l2, lsem)
    more.middle()
    more.arrive()
    last_out[...] = rows_of(l2)
    Flow.drain(flows)
    scatter.drain()
    sums.drain()
    norms.drain()
    more.drain()


def final_kernel(
    dims, yx, yw, zx, zw, diag, mix, ritz, norm_in, ritz_out, search_out, norms_out,
    xs, ss, nsum, nland, ns,
):
    place = Place(dims)
    barrier, count = place.enter(False)
    vectors, _, search, squares = moved_on(
        yx[...], yw[...], zx[...], zw[...], mix[...], ritz[...], diag[...]
    )
    nsum[...] = jnp.broadcast_to(squares, (8, V))
    pl.semaphore_wait(barrier, count)
    norms = Spread(place, lambda x, core: nsum, lambda i: nland.at[i], ns)
    xs[...] = vectors
    ss[...] = search
    own = pl.ds(pl.multiple_of((place.z * dims[1] + place.y) * Q, Q), Q)
    ritz_out[...] = xs[own, :]
    search_out[...] = ss[own, :]
    norms.arrive()
    squares = nsum[...]
    for i in range(1, 2 * dims[3]):
        squares = squares + nland[i]
    norms_out[0:1, :] = norm_in[0:1, :]
    norms_out[1:2, :] = jnp.sqrt(squares)[0:1, :]
    norms.drain()


def vmem(count):
    return [pl.BlockSpec(memory_space=pltpu.VMEM)] * count


def shapes(*sizes):
    return tuple(jax.ShapeDtypeStruct(s, f32) for s in sizes)


def communicating(body, dims, number, in_specs, outs, scratch):
    return pl.pallas_call(
        functools.partial(body, dims),
        out_shape=outs,
        in_specs=in_specs,
        out_specs=tuple(vmem(len(outs))),
        scratch_shapes=scratch,
        compiler_params=pltpu.CompilerParams(collective_id=number, has_side_effects=True),
    )


def per_device(dims, kernel, ritz_block, search_block, precond_diag):
    nz, ny, _, nx = dims
    height, group, rows = nz * ny * Q, 2 * nx, nx * Q
    tall = (height, V)
    grid = pltpu.VMEM((nz, ny, Q, V), f32)
    entries = jnp.pad(precond_diag, (0, V - Q)).reshape(1, V)
    metric, projected, yx, yw, zx, zw, kern, diag = communicating(
        images_kernel,
        dims,
        0,
        [pl.BlockSpec(memory_space=pl.ANY)] * 4,
        shapes((3 * V, V), (3 * V, V), tall, tall, tall, tall, (2, rows, height), tall),
        [grid] * 4
        + [
            pltpu.VMEM((nz, ny, 1, V), f32),
            pltpu.VMEM((rows, 2 * height), f32),
            pltpu.VMEM((2, rows, height), f32),
            pltpu.VMEM((rows, height), f32),
            pltpu.VMEM((2, nx, Q, 2 * V), f32),
            pltpu.VMEM((group, Q, 2 * V), f32),
        ]
        + sum_scratch(group, 3 * V // group) * 2
        + [pltpu.SemaphoreType.DMA((4,)), pltpu.SemaphoreType.DMA((2,))]
        + [flow_sems() for _ in range(5)]
        + [near_sems()],
    )(kernel.reshape(rows, 2 * height), ritz_block, search_block, entries)
    mix, ritz = coefficients(True, metric, projected)
    sums, last, norm, xx, kx, ww, kw = communicating(
        search_kernel,
        dims,
        1,
        vmem(8),
        shapes((3 * V, V), (V, V), (8, V), tall, tall, tall, tall),
        [
            pltpu.VMEM((2, nx, Q, V), f32),
            pltpu.VMEM((group, Q, V), f32),
            grid,
        ]
        + sum_scratch(group, 3 * V // group)
        + sum_scratch(group, V // group)
        + [
            pltpu.VMEM((8, V), f32),
            pltpu.VMEM((group, 8, V), f32),
        ]
        + [flow_sems() for _ in range(2)]
        + [near_sems() for _ in range(2)],
    )(yx, yw, zx, zw, kern, diag, mix, ritz)
    mix, ritz = coefficients(False, sums, last, ritz)
    return communicating(
        final_kernel,
        dims,
        2,
        vmem(8),
        shapes((Q, V), (Q, V), (2, V)),
        [
            pltpu.VMEM(tall, f32),
            pltpu.VMEM(tall, f32),
            pltpu.VMEM((8, V), f32),
            pltpu.VMEM((group, 8, V), f32),
            near_sems(),
        ],
    )(xx, ww, kx, kw, diag, mix, ritz, norm)


def solution(mesh):
    chips, cols = mesh.shape["blk"] // 2, mesh.shape["col"]
    ny = min(8, chips // 2)
    dims = (chips // ny, ny, 2, cols)
    torus = Mesh(mesh.devices.reshape(dims), BLK_COL)
    placed = (P(BLK, "col", None), P(BLK_COL, None), P(BLK_COL, None), P(BLK_COL))
    return jax.shard_map(
        functools.partial(per_device, dims),
        mesh=torus,
        in_specs=placed,
        out_specs=(P(BLK_COL, None), P(BLK_COL, None), P()),
        check_vma=False,
    )
```

time: 502 us -> 162 us (0.32); the launches traced: 496 us -> 162 us
  other arithmetic: 157 us -> 0 us
  Pallas kernels: 0 us -> 155 us
  waiting for transfers between devices: 149 us -> 0 us
  blocking collectives: 98.3 us -> 0 us
  starting transfers between devices: 33.3 us -> 0 us
  matrix products: 21.1 us -> 0 us
  between operations: 17.8 us -> 0.67 us
  local copies, waits for them, and re-layouts: 19.3 us -> 5.67 us
    pallas_call x0 -> x5, Pallas kernels: none -> 155 us  [the longest x1 74.4 us: per_device(): communicating(images_kernel, dims, 0, [pl.BlockSpec(memory_space=pl.ANY)]...]
    another operation x29 -> x0, other arithmetic: 155 us -> none  [the longest x13 68.6 us: coefficients(): lower_metric = jnp.linalg.cholesky(metric)]
    all_to_all x7 -> x0, blocking collectives: 98.3 us -> none  [the longest x2 35.9 us: sum_by_axis(): return jnp.sum(lax.all_to_all(own, far, 0, 0, tiled=True), axis=0)]
    all_gather x1 -> x0, waiting for transfers between devices: 89.4 us -> none  [side_by_side(): out, at, done = (lax.all_gather(both, axis, axis=dim, tiled=True), 0, [])]
    all_to_all x7 -> x0, waiting for transfers between devices: 59.6 us -> none  [the longest x5 51.4 us: sent_to_all(): lax.all_to_all(jnp.broadcast_to(value[None], (length, *value.shape)), axi...]
    all_to_all x7 -> x0, starting transfers between devices: 33.3 us -> none  [the longest x5 25.9 us: sent_to_all(): lax.all_to_all(jnp.broadcast_to(value[None], (length, *value.shape)), axi...]
    dot_general x31 -> x0, matrix products: 16.5 us -> none  [the longest x3 5.87 us: accumulate(): jnp.dot(kernel_rows, segment, precision=highest, preferred_element_type=j...]
    another operation x23 -> x0, local copies, waits for them, and re-layouts: 9.23 us -> none  [the longest x15 8.1 us: coefficients(): lax.linalg.triangular_solve(lower_metric, halfway, left_side=True, lower=...]
  transfers between devices with their start and end apart: 8 -> 0, of which waited for: 8 -> 0; matrix products, arithmetic and copies ran while one was open for 1% -> 0% of each run, Pallas kernels for 0% -> 0%
where the time goes in v1:
time: 162 us
  Pallas kernels  155 us (96%)
  local copies, waits for them, and re-layouts  5.67 us (4%)
    pallas_call x1, Pallas kernels, per_device(): communicating(images_kernel, dims, 0, [pl.BlockSpec(memory_space=pl.ANY)]...  74.4 us
    pallas_call x1, Pallas kernels, per_device(): communicating(search_kernel, dims, 1, vmem(8), shapes((3 * V, V), (V, V),...  40 us
    pallas_call x2, Pallas kernels, coefficients(): pl.pallas_call(functools.partial(coefficients_kernel, first), out_shape=(...  32.5 us
    pallas_call x1, Pallas kernels, per_device(): communicating(final_kernel, dims, 2, vmem(8), shapes((Q, V), (Q, V), (2,...  8.4 us
    unnamed x8, local copies, waits for them, and re-layouts  4.5 us

profile of v1, /device:TPU:1, one launch (start us, length us, event | category | flops | bytes accessed | tf_op | source)
XLA Modules:
  0.0 161.7 jit_solution(12691978151260220850)
XLA Ops:
  0.6 1.2 pad_bitcast_fusion.d_in
  1.8 2.0 %copy.9 = f32[64,1,2048]{2,0,1:T(8,128)} copy(f32[64,1,2048]{2,1,0:T(1,128)} %param.4) | data formatting | bytes 1048576
  3.8 74.4 %shard_map.67 = (f32[384,128]{1,0:T(8,128)}, f32[384,128]{1,0:T(8,128)}, f32[1024,128]{1,0:T(8,128)}, f32[1024,128]{1,0:T(8,128)}, f32[1024,128]{1,0:T(8,128)}, ...) custom-call(f32[64,2048]{1,0:T(8,128)} %bitcast.5, f32[16,128]{1,0:T(8,128)} %x_in.1, ...), custom_call_target="tpu_custom_call" | custom-call | tf_op jit(solution)/shard_map/pallas_call | solution.py:542
  78.2 18.9 %shard_map.68 = (f32[256,128]{1,0:T(8,128)}, f32[128,128]{1,0:T(8,128)}) custom-call(f32[384,128]{1,0:T(8,128)} %get-tuple-element.28.refs_0_, f32[384,128]{1,0:T(8,128)} %get-tuple-element.29.refs_1_), custom_call_target="tpu_custom_call" | custom-call | tf_op jit(solution)/shard_map/pallas_call | solution.py:117
  97.1 40.0 %shard_map.69 = (f32[384,128]{1,0:T(8,128)}, f32[128,128]{1,0:T(8,128)}, f32[8,128]{1,0:T(8,128)}, f32[1024,128]{1,0:T(8,128)}, f32[1024,128]{1,0:T(8,128)}, /*index=5*/f32[1024,128]{1,0:T(8,128)}, f32[1024,128]{1,0:T(8,128)}) custom-call(f32[1024,128]{1,0:T(8,128)} %get-tuple-element.22.yx, f32[1024,128]{1,0:T(8,128)} %get-tuple-element.23.yw, ...), custom_call_target="tpu_custom_call" | custom-call | tf_op jit(solution)/shard_map/pallas_call | solution.py:563
  137.1 13.7 %shard_map.70 = (f32[256,128]{1,0:T(8,128)}, f32[128,128]{1,0:T(8,128)}) custom-call(f32[384,128]{1,0:T(8,128)} %get-tuple-element.36.refs_0_, f32[128,128]{1,0:T(8,128)} %get-tuple-element.37.refs_1_, f32[128,128]{1,0:T(8,128)} %get-tuple-element.31.ritz.refs_2_), custom_call_target="tpu_custom_call" | custom-call | tf_op jit(solution)/shard_map/pallas_call | solution.py:117
  150.8 8.4 %shard_map.71 = (f32[16,128]{1,0:T(8,128)}, f32[16,128]{1,0:T(8,128)}, f32[2,128]{1,0:T(2,128)}) custom-call(f32[1024,128]{1,0:T(8,128)} %get-tuple-element.32.yx, f32[1024,128]{1,0:T(8,128)} %get-tuple-element.33.yw, f32[1024,128]{1,0:T(8,128)} %get-tuple-element.34.zx, f32[1024,128]{1,0:T(8,128)} %get-tuple-element.35.zw, ...), custom_call_target="tpu_custom_call" | custom-call | tf_op jit(solution)/shard_map/pallas_call | solution.py:584
  159.2 0.0 copy-start
  159.2 1.3 copy.13
  160.5 0.0 copy-done
  160.5 0.0 copy-start.1
  160.5 0.6 copy.14
  161.1 0.0 copy-done.1
  161.1 0.6 copy.15
Async XLA Ops:
  159.2 1.3 copy-start
  160.5 0.6 copy-start.1

commit v2 on v1

v2 whole, which is shorter than its diff:
```python
import functools

import jax
import jax.numpy as jnp
from jax import lax
from jax.experimental import pallas as pl
from jax.experimental.pallas import tpu as pltpu
from jax.sharding import Mesh
from jax.sharding import PartitionSpec as P

MESH = pl.DeviceIdType.MESH
BLK = ("blk_0", "blk_1", "blk_2")
BLK_COL = ("blk_0", "blk_1", "blk_2", "col")
V = 128
Q = 16
PANEL = 16
f32 = jnp.float32
bf16 = jnp.bfloat16
highest = lax.Precision.HIGHEST


def dot(a, b, ca=1, cb=0):
    return lax.dot_general(
        a, b, (((ca,), (cb,)), ((), ())), precision=highest, preferred_element_type=f32
    )


def split(a):
    high = a.astype(bf16)
    return high, (a - high.astype(f32)).astype(bf16)


def dot3(a, b, ca=1, cb=0):
    dims = (((ca,), (cb,)), ((), ()))

    def one(x, y):
        return lax.dot_general(x, y, dims, preferred_element_type=f32)

    return one(a[0], b[0]) + (one(a[0], b[1]) + one(a[1], b[0]))


def inverse_factor(matrix, work):
    row = lax.broadcasted_iota(jnp.int32, (V, V), 0)
    lane = lax.broadcasted_iota(jnp.int32, (V, V), 1)
    work[:, :V] = matrix
    work[:, V:] = jnp.where(row == lane, 1.0, 0.0).astype(f32)
    sub = lax.broadcasted_iota(jnp.int32, (PANEL, V), 0)
    for start in range(0, V, PANEL):
        end = start + PANEL
        left = work[start:end, :V]
        right = work[start:end, V:]
        columns = [
            jnp.broadcast_to(left[:, start + t : start + t + 1], (PANEL, V)) for t in range(PANEL)
        ]
        scale = jnp.zeros((PANEL, V), f32)
        for r in range(PANEL):
            inverse = lax.rsqrt(jnp.broadcast_to(columns[r][r : r + 1, :], (PANEL, V)))
            scale = jnp.where(sub == r, inverse, scale)
            if r == PANEL - 1:
                break
            factor = jnp.where(sub > r, columns[r] * inverse, 0.0)
            for t in range(r + 1, PANEL):
                columns[t] = columns[t] - factor * factor[t : t + 1, :]
            factor = factor * inverse
            left = left - factor * left[r : r + 1, :]
            right = right - factor * right[r : r + 1, :]
        left = left * scale
        right = right * scale
        work[start:end, V:] = right
        if end < V:
            lower = dot(left, jnp.concatenate([left, right], 1), 0, 0)
            work[end:, :] = work[end:, :] - lower[end:, :]
    return work[:, V:]


class Place:
    def __init__(self, dims):
        self.dims = dims
        self.z, self.y, self.core, self.x = (lax.axis_index(a) for a in BLK_COL)

    def plane(self, axis, step):
        name = ("blk_0", "blk_1")[axis]
        size = self.dims[axis]
        here = (self.z, self.y)[axis]
        return {name: lax.rem(here + step + size, size)}

    def near(self, index):
        dx, dc = index // 2, index % 2
        x = lax.rem(self.x + dx, self.dims[3])
        core = lax.rem(self.core + dc, 2)
        return x, core, {"col": x, "blk_2": core}

    def group(self):
        return self.x * 2 + self.core

    def enter(self, plane):
        barrier = pltpu.get_barrier_semaphore()
        count = 0
        peers = [self.near(i)[2] for i in range(1, 2 * self.dims[3])]
        if plane:
            for axis in range(2):
                peers += [self.plane(axis, s) for s in range(1, self.dims[axis])]
        for peer in peers:
            pl.semaphore_signal(barrier, inc=1, device_id=peer, device_id_type=MESH)
            count += 1
        return barrier, count


def remote(src, dst, send, recv, to):
    return pltpu.make_async_remote_copy(
        src_ref=src,
        dst_ref=dst,
        send_sem=send,
        recv_sem=recv,
        device_id=to,
        device_id_type=MESH,
    )


class Flow:
    def __init__(self, place, buffer, rows, first, sems):
        self.place, self.buffer, self.rows, self.first = place, buffer, rows, first
        self.second = 1 - first
        self.near = Flow.steps(place.dims[first])
        self.far = Flow.steps(place.dims[self.second])[::-1]
        self.send, self.receive = sems
        self.sent = []
        here = (place.z, place.y)
        self.here, self.there = here[first], here[self.second]

    @staticmethod
    def steps(size):
        return sorted((d if d <= size // 2 else d - size for d in range(1, size)), key=abs)

    def start(self, ref, number, axis, step):
        copy = remote(
            ref,
            ref,
            self.send.at[len(self.sent)],
            self.receive.at[number],
            self.place.plane(axis, step),
        )
        copy.start()
        self.sent.append(copy)
        return copy

    def block(self, here, there):
        at = (here, there) if self.first == 0 else (there, here)
        return self.buffer.at[at[0], at[1], self.rows]

    def fan(self, here):
        for i, step in enumerate(self.far):
            self.start(self.block(here, self.there), len(self.near) + i, self.second, step)

    def begin(self):
        own = self.block(self.here, self.there)
        self.first_copies = [
            self.start(own, i, self.first, step) for i, step in enumerate(self.near)
        ]
        self.fan(self.here)

    def relay(self, i):
        self.first_copies[i].wait_recv()
        size = self.place.dims[self.first]
        self.fan(lax.rem(self.here - self.near[i] + size, size))

    def end(self):
        size = self.place.dims[self.second]
        for i, step in enumerate(self.far):
            origin = lax.rem(self.there - step + size, size)
            if self.first == 0:
                line = self.buffer.at[:, origin, self.rows]
            else:
                line = self.buffer.at[origin, :, self.rows]
            number = len(self.near) + i
            remote(
                line,
                line,
                self.send.at[0],
                self.receive.at[number],
                self.place.plane(self.second, step),
            ).wait_recv()

    @staticmethod
    def relays(flows):
        for i in range(max(len(f.near) for f in flows)):
            for flow in flows:
                if i < len(flow.near):
                    flow.relay(i)

    @staticmethod
    def ends(flows):
        for flow in flows:
            flow.end()

    @staticmethod
    def drain(flows):
        for flow in flows:
            for copy in flow.sent:
                copy.wait_send()


def flow_sems(dims):
    nz, ny = dims[:2]
    return [
        pltpu.SemaphoreType.DMA((nz * ny + max(nz, ny),)),
        pltpu.SemaphoreType.DMA((nz + ny,)),
    ]


class Spread:
    def __init__(self, place, source, target, sems):
        self.place = place
        self.copies = []
        for i in range(1, 2 * place.dims[3]):
            x, core, to = place.near(i)
            self.copies.append(
                remote(source(x, core), target(i), sems.at[0, i], sems.at[1, i], to)
            )
        for copy in self.copies:
            copy.start()

    def arrive(self):
        for copy in self.copies:
            copy.wait_recv()

    def drain(self):
        for copy in self.copies:
            copy.wait_send()


class Sum:
    def __init__(self, place, value, pieces, landed, whole, sems):
        self.place, self.pieces, self.landed, self.whole = place, pieces, landed, whole
        self.sems = sems
        pieces[...] = value.reshape(pieces.shape)
        self.scatter = Spread(
            place, lambda x, core: pieces.at[x * 2 + core], lambda i: landed.at[i], sems.at[0]
        )

    def middle(self):
        place, own = self.place, self.place.group()
        self.scatter.arrive()
        total = self.pieces[own]
        for i in range(1, 2 * place.dims[3]):
            total = total + self.landed[i]
        self.whole[own] = total
        self.share = Spread(
            place,
            lambda x, core: self.whole.at[own],
            lambda i: self.whole.at[own],
            self.sems.at[1],
        )

    def arrive(self):
        self.share.arrive()

    def drain(self):
        self.scatter.drain()
        self.share.drain()


def near_sems(*lead):
    return pltpu.SemaphoreType.DMA((*lead, 2, 8))


def sum_scratch(group, rows):
    return [pltpu.VMEM((group, rows, V), f32)] * 3 + [near_sems(2)]


def rows_of(buffer):
    return buffer[...].reshape(-1, buffer.shape[-1])


def three(gram):
    return jnp.concatenate([gram[:V, :V], gram[:V, V:], gram[V:, V:]], 0)


def metric_factor(metric, work):
    xx, xw, ww = (metric[i * V : (i + 1) * V, :] for i in range(3))
    top = inverse_factor(xx, work)
    side = dot(top, xw)
    low = inverse_factor(ww - dot(side, side, 0, 0), work)
    cross = -dot(dot(low, side, 1, 1), top)
    zero = jnp.zeros((V, V), f32)
    return jnp.concatenate(
        [jnp.concatenate([top, zero], 1), jnp.concatenate([cross, low], 1)], 0
    )


def first_mixing(factor, projected, work):
    xx, xw, ww = (projected[i * V : (i + 1) * V, :] for i in range(3))
    left = jnp.concatenate([xx, xw.T], 0)
    whole = jnp.concatenate([left, jnp.concatenate([xw, ww], 0)], 1)
    half = dot(factor, left)
    power = dot(factor, half, 0, 0)
    applied = dot(whole, power)
    back = inverse_factor(dot(half, half, 0, 0), work)
    mix = dot(power, back, 1, 1)
    return mix, dot(mix, dot(applied, back, 1, 1), 0, 0)


def second_mixing(sums, ritz, work):
    xw, ww, image = (sums[i * V : (i + 1) * V, :] for i in range(3))
    low = inverse_factor(ww - dot(xw, xw, 0, 0), work)
    lower = dot(low, image.T - dot(xw, ritz, 0, 0))
    back = inverse_factor(dot(ritz, ritz, 0, 0) + dot(lower, lower, 0, 0), work)
    lower = dot(low, dot(lower, back, 1, 1), 0, 0)
    upper = dot(ritz, back, 1, 1) - dot(xw, lower)
    return jnp.concatenate([upper, lower], 0)


def correction_of(images, vectors, ritz, diag):
    row = lax.broadcasted_iota(jnp.int32, (V, V), 0)
    lane = lax.broadcasted_iota(jnp.int32, (V, V), 1)
    values = jnp.sum(jnp.where(row == lane, ritz, 0.0), axis=0, keepdims=True)
    residual = images - dot3(vectors, split(ritz))
    squares = jnp.sum(residual * residual, axis=0, keepdims=True)
    return residual / jnp.maximum(jnp.abs(diag - values), 1.0), squares


def davidson_kernel(
    dims, k_in, x_in, w_in, d_in, ritz_out, search_out, norms_out,
    gx, gw, hx, hw, hk, gd, entry, kraw, kown, kland, part, landed, less, lessland,
    m0, m1, m2, msem, p0, p1, p2, psem, q0, q1, q2, qsem, l0, l1, l2, lsem,
    nsum, nland, osum, oland, xs, ss, work,
    load, ksem, ax, bx, aw, bw, cx, dx, cw, dw, ek, fk, gk, ik, ad, bd, rs, ts, ns, os,
):
    place = Place(dims)
    nz, ny, _, nx = dims
    group = 2 * nx
    barrier, count = place.enter(True)
    loads = [
        pltpu.make_async_copy(x_in, gx.at[place.z, place.y], load.at[0]),
        pltpu.make_async_copy(w_in, gw.at[place.z, place.y], load.at[1]),
        pltpu.make_async_copy(d_in, gd.at[place.z, place.y], load.at[2]),
        pltpu.make_async_copy(k_in, kraw, load.at[3]),
    ]
    for copy in loads:
        copy.start()
    for copy in loads[:3]:
        copy.wait()
    pl.semaphore_wait(barrier, count)
    flows = [
        Flow(place, gx, slice(None), 1, (ax, bx)),
        Flow(place, gw, slice(None), 0, (aw, bw)),
    ]
    for flow in flows:
        flow.begin()
    Flow.relays(flows)
    small = Flow(place, gd, slice(None), 1, (ad, bd))
    small.begin()
    loads[3].wait()
    i = lax.broadcasted_iota(jnp.int32, (2 * V, 2 * V), 0)
    j = lax.broadcasted_iota(jnp.int32, (2 * V, 2 * V), 1)
    to = ((i // Q) % 2) * V + (i // (2 * Q)) * Q + i % Q
    mover = jnp.where(j == to, 1.0, 0.0).astype(f32)
    for tile in range(kraw.shape[1] // (2 * V)):
        moved = dot(kraw[:, tile * 2 * V : (tile + 1) * 2 * V], mover)
        kown[0, :, tile * V : (tile + 1) * V] = moved[:, :V]
        kown[1, :, tile * V : (tile + 1) * V] = moved[:, V:]
    swap = remote(kown.at[1 - place.core], kland, ksem.at[0], ksem.at[1], place.near(1)[2])
    swap.start()
    Flow.relays([small])
    swap.wait()
    both = split(jnp.concatenate([kown[place.core], kland[...]], 0))
    rows = kland.shape[0]
    Flow.ends(flows)
    ys = split(jnp.concatenate([rows_of(gx), rows_of(gw)], 1))
    image = dot3(both, ys)
    part[place.core] = image[:rows].reshape(nx, Q, 2 * V)
    part[1 - place.core] = image[rows:].reshape(nx, Q, 2 * V)
    scatter = Spread(place, lambda x, core: part.at[core, x], lambda i: landed.at[i], rs)
    sums = Sum(place, three(dot3(ys, ys, 0, 0)), m0, m1, m2, msem)
    scatter.arrive()
    total = part[place.core, place.x]
    for i in range(1, group):
        total = total + landed[i]
    hx[place.z, place.y] = total[:, :V]
    hw[place.z, place.y] = total[:, V:]
    again = [
        Flow(place, hx, slice(None), 1, (cx, dx)),
        Flow(place, hw, slice(None), 0, (cw, dw)),
    ]
    for flow in again:
        flow.begin()
    sums.middle()
    Flow.relays(again)
    small.end()
    height = nz * ny * Q
    r = lax.broadcasted_iota(jnp.int32, (height, nz * ny), 0)
    b = lax.broadcasted_iota(jnp.int32, (height, nz * ny), 1)
    pick = jnp.where(r // Q == b, 1.0, 0.0).astype(f32)
    entries = dot(pick, gd[...].reshape(nz * ny, V))
    r = lax.broadcasted_iota(jnp.int32, (height, V), 0)
    b = lax.broadcasted_iota(jnp.int32, (height, V), 1)
    entry[...] = dot(jnp.where(r % Q == b, entries, 0.0), jnp.ones((V, V), f32))
    sums.arrive()
    factor = metric_factor(rows_of(m2), work)
    Flow.ends(again)
    zs = split(jnp.concatenate([rows_of(hx), rows_of(hw)], 1))
    more = Sum(place, three(dot3(ys, zs, 0, 0)), p0, p1, p2, psem)
    more.middle()
    more.arrive()
    mix, ritz = first_mixing(factor, rows_of(p2), work)
    mixes = split(mix)
    vectors, images = dot3(ys, mixes), dot3(zs, mixes)
    vs = split(vectors)
    search, squares = correction_of(images, vs, ritz, entry[...])
    ws = split(search)
    image = dot3(both, ws)
    less[place.core] = image[:rows].reshape(nx, Q, V)
    less[1 - place.core] = image[rows:].reshape(nx, Q, V)
    rescatter = Spread(place, lambda x, core: less.at[core, x], lambda i: lessland.at[i], ts)
    us = split(images)
    gram = jnp.concatenate([dot3(a, ws, 0, 0) for a in (vs, ws, us)], 0)
    cross = Sum(place, gram, q0, q1, q2, qsem)
    nsum[...] = jnp.broadcast_to(squares, (8, V))
    norms = Spread(place, lambda x, core: nsum, lambda i: nland.at[i], ns)
    rescatter.arrive()
    total = less[place.core, place.x]
    for i in range(1, group):
        total = total + lessland[i]
    hk[place.z, place.y] = total
    last = [
        Flow(place, hk, slice(0, Q // 2), 1, (ek, fk)),
        Flow(place, hk, slice(Q // 2, Q), 0, (gk, ik)),
    ]
    for flow in last:
        flow.begin()
    cross.middle()
    Flow.relays(last)
    cross.arrive()
    mixes = split(second_mixing(rows_of(q2), ritz, work))
    pair = tuple(jnp.concatenate([a, b], 1) for a, b in zip(vs, ws))
    vectors = dot3(pair, mixes)
    vs = split(vectors)
    xs[...] = vectors
    own = pl.ds(pl.multiple_of((place.z * ny + place.y) * Q, Q), Q)
    ritz_out[...] = xs[own, :]
    norms.arrive()
    squares = nsum[...]
    for i in range(1, group):
        squares = squares + nland[i]
    norms_out[0:1, :] = jnp.sqrt(squares)[0:1, :]
    Flow.ends(last)
    ks = split(rows_of(hk))
    images = dot3(tuple(jnp.concatenate([a, b], 1) for a, b in zip(us, ks)), mixes)
    values = Sum(place, dot3(vs, split(images), 0, 0), l0, l1, l2, lsem)
    values.middle()
    values.arrive()
    search, squares = correction_of(images, vs, rows_of(l2), entry[...])
    osum[...] = jnp.broadcast_to(squares, (8, V))
    final = Spread(place, lambda x, core: osum, lambda i: oland.at[i], os)
    ss[...] = search
    search_out[...] = ss[own, :]
    Flow.drain(flows + [small] + again + last)
    for other in (scatter, sums, more, rescatter, cross, norms, values):
        other.drain()
    final.arrive()
    squares = osum[...]
    for i in range(1, group):
        squares = squares + oland[i]
    norms_out[1:2, :] = jnp.sqrt(squares)[0:1, :]
    final.drain()


def per_device(dims, kernel, ritz_block, search_block, precond_diag):
    nz, ny, _, nx = dims
    height, group, rows = nz * ny * Q, 2 * nx, nx * Q
    grid = pltpu.VMEM((nz, ny, Q, V), f32)
    entries = jnp.pad(precond_diag, (0, V - Q)).reshape(1, V)
    small = [pltpu.VMEM((8, V), f32), pltpu.VMEM((group, 8, V), f32)]
    scratch = [grid] * 5 + [
        pltpu.VMEM((nz, ny, 1, V), f32),
        pltpu.VMEM((height, V), f32),
        pltpu.VMEM((rows, 2 * height), f32),
        pltpu.VMEM((2, rows, height), f32),
        pltpu.VMEM((rows, height), f32),
        pltpu.VMEM((2, nx, Q, 2 * V), f32),
        pltpu.VMEM((group, Q, 2 * V), f32),
        pltpu.VMEM((2, nx, Q, V), f32),
        pltpu.VMEM((group, Q, V), f32),
    ]
    scratch += sum_scratch(group, 3 * V // group) * 3 + sum_scratch(group, V // group)
    scratch += small * 2 + [pltpu.VMEM((height, V), f32)] * 2 + [pltpu.VMEM((V, 2 * V), f32)]
    scratch += [pltpu.SemaphoreType.DMA((4,)), pltpu.SemaphoreType.DMA((2,))]
    for _ in range(7):
        scratch += flow_sems(dims)
    scratch += [near_sems() for _ in range(4)]
    return pl.pallas_call(
        functools.partial(davidson_kernel, dims),
        out_shape=tuple(jax.ShapeDtypeStruct(s, f32) for s in ((Q, V), (Q, V), (2, V))),
        in_specs=[pl.BlockSpec(memory_space=pl.ANY)] * 4,
        out_specs=(pl.BlockSpec(memory_space=pltpu.VMEM),) * 3,
        scratch_shapes=scratch,
        compiler_params=pltpu.CompilerParams(collective_id=0, has_side_effects=True),
    )(kernel.reshape(rows, 2 * height), ritz_block, search_block, entries)


def solution(mesh):
    chips, cols = mesh.shape["blk"] // 2, mesh.shape["col"]
    ny = min(8, chips // 2)
    dims = (chips // ny, ny, 2, cols)
    torus = Mesh(mesh.devices.reshape(dims), BLK_COL)
    placed = (P(BLK, "col", None), P(BLK_COL, None), P(BLK_COL, None), P(BLK_COL))
    return jax.shard_map(
        functools.partial(per_device, dims),
        mesh=torus,
        in_specs=placed,
        out_specs=(P(BLK_COL, None), P(BLK_COL, None), P()),
        check_vma=False,
    )
```

time: 162 us -> 125 us (0.77)
  Pallas kernels: 155 us -> 119 us
    pallas_call x5 -> x1, Pallas kernels: 155 us -> 119 us  [per_device(): pl.pallas_call(functools.partial(davidson_kernel, dims), out_shape=tuple(...]
where the time goes in v2:
time: 125 us
  Pallas kernels  119 us (95%)
  local copies, waits for them, and re-layouts  5.69 us (5%)
    pallas_call x1, Pallas kernels, per_device(): pl.pallas_call(functools.partial(davidson_kernel, dims), out_shape=tuple(...  119 us
    unnamed x8, local copies, waits for them, and re-layouts  4.52 us

profile of v2, /device:TPU:1, one launch (start us, length us, event | category | flops | bytes accessed | tf_op | source)
XLA Modules:
  0.0 124.9 jit_solution(17628960803330055277)
XLA Ops:
  0.6 1.2 pad_bitcast_fusion.d_in
  1.8 2.0 %copy.9 = f32[64,1,2048]{2,0,1:T(8,128)} copy(f32[64,1,2048]{2,1,0:T(1,128)} %param.4) | data formatting | bytes 1048576
  3.8 118.6 %shard_map.67 = (f32[16,128]{1,0:T(8,128)}, f32[16,128]{1,0:T(8,128)}, f32[2,128]{1,0:T(2,128)}) custom-call(f32[64,2048]{1,0:T(8,128)} %bitcast.5, f32[16,128]{1,0:T(8,128)} %x_in.1, f32[16,128]{1,0:T(8,128)} %w_in.1, f32[1,128]{1,0:T(1,128)} %pad_bitcast_fusion.d_in), custom_call_target="tpu_custom_call" | custom-call | tf_op jit(solution)/shard_map/pallas_call | solution.py:491
  122.4 0.0 copy-start
  122.4 1.3 %copy.13 = f32[16,128]{1,0:T(8,128)} copy(f32[16,128]{1,0:T(8,128)} %get-tuple-element.6) | data formatting | bytes 16384
  123.7 0.0 copy-done
  123.7 0.0 copy-start.1
  123.7 0.6 copy.14
  124.3 0.1 copy-done.1
  124.3 0.6 copy.15
Async XLA Ops:
  122.4 1.3 %copy-start = (f32[16,128]{1,0:T(8,128)S(1)}, f32[16,128]{1,0:T(8,128)}, u32[]{:S(2)}) copy-start(f32[16,128]{1,0:T(8,128)} %get-tuple-element.7) | copy-start | bytes 24580
  123.7 0.7 copy-start.1

commit v3 on v2

--- a/solution.py
+++ b/solution.py
@@ -13,7 +13,7 @@
 BLK_COL = ("blk_0", "blk_1", "blk_2", "col")
 V = 128
 Q = 16
-PANEL = 16
+PANEL = 32
 f32 = jnp.float32
 bf16 = jnp.bfloat16
 highest = lax.Precision.HIGHEST
@@ -200,6 +200,34 @@
                 copy.wait_send()
 
 
+class Lines:
+    def __init__(self, place, buffer, send, receive):
+        self.place, self.buffer, self.send, self.receive = place, buffer, send, receive
+        self.copies = []
+        self.start(buffer.at[place.z, place.y], 1)
+
+    def start(self, ref, axis):
+        at = len(self.copies)
+        for i, step in enumerate(Flow.steps(self.place.dims[axis])):
+            peer = self.place.plane(axis, step)
+            copy = remote(ref, ref, self.send.at[at + i], self.receive.at[at + i], peer)
+            copy.start()
+            self.copies.append(copy)
+        self.pending = self.copies[at:]
+
+    def middle(self):
+        self.arrive()
+        self.start(self.buffer.at[self.place.z], 0)
+
+    def arrive(self):
+        for copy in self.pending:
+            copy.wait_recv()
+
+    def drain(self):
+        for copy in self.copies:
+            copy.wait_send()
+
+
 def flow_sems(dims):
     nz, ny = dims[:2]
     return [
@@ -288,16 +316,17 @@
     )
 
 
-def first_mixing(factor, projected, work):
-    xx, xw, ww = (projected[i * V : (i + 1) * V, :] for i in range(3))
+def first_mixing(factor, projected, rest, work):
+    xx, xw = projected[:V, :], projected[V:, :]
     left = jnp.concatenate([xx, xw.T], 0)
-    whole = jnp.concatenate([left, jnp.concatenate([xw, ww], 0)], 1)
     half = dot(factor, left)
     power = dot(factor, half, 0, 0)
-    applied = dot(whole, power)
+    rest.middle()
     back = inverse_factor(dot(half, half, 0, 0), work)
+    rest.arrive()
+    whole = jnp.concatenate([left, jnp.concatenate([xw, rows_of(rest.whole)], 0)], 1)
     mix = dot(power, back, 1, 1)
-    return mix, dot(mix, dot(applied, back, 1, 1), 0, 0)
+    return mix, dot(mix, dot(whole, mix), 0, 0)
 
 
 def second_mixing(sums, ritz, work):
@@ -310,19 +339,19 @@
     return jnp.concatenate([upper, lower], 0)
 
 
-def correction_of(images, vectors, ritz, diag):
+def correction_of(images, moved, ritz, diag):
     row = lax.broadcasted_iota(jnp.int32, (V, V), 0)
     lane = lax.broadcasted_iota(jnp.int32, (V, V), 1)
     values = jnp.sum(jnp.where(row == lane, ritz, 0.0), axis=0, keepdims=True)
-    residual = images - dot3(vectors, split(ritz))
+    residual = images - moved
     squares = jnp.sum(residual * residual, axis=0, keepdims=True)
     return residual / jnp.maximum(jnp.abs(diag - values), 1.0), squares
 
 
 def davidson_kernel(
     dims, k_in, x_in, w_in, d_in, ritz_out, search_out, norms_out,
-    gx, gw, hx, hw, hk, gd, entry, kraw, kown, kland, part, landed, less, lessland,
-    m0, m1, m2, msem, p0, p1, p2, psem, q0, q1, q2, qsem, l0, l1, l2, lsem,
+    gx, gw, hx, hw, hk, gd, dsm, entry, kraw, kown, kland, part, landed, less, lessland,
+    m0, m1, m2, msem, p0, p1, p2, psem, r0, r1, r2, rsem, q0, q1, q2, qsem, l0, l1, l2, lsem,
     nsum, nland, osum, oland, xs, ss, work,
     load, ksem, ax, bx, aw, bw, cx, dx, cw, dw, ek, fk, gk, ik, ad, bd, rs, ts, ns, os,
 ):
@@ -330,11 +359,12 @@
     nz, ny, _, nx = dims
     group = 2 * nx
     barrier, count = place.enter(True)
+    taps = pltpu.make_async_copy(d_in, dsm, load.at[2])
     loads = [
         pltpu.make_async_copy(x_in, gx.at[place.z, place.y], load.at[0]),
         pltpu.make_async_copy(w_in, gw.at[place.z, place.y], load.at[1]),
-        pltpu.make_async_copy(d_in, gd.at[place.z, place.y], load.at[2]),
-        pltpu.make_async_copy(k_in, kraw, load.at[3]),
+        taps,
+        pltpu.make_async_copy(k_in.at[:, 0], kraw, load.at[3]),
     ]
     for copy in loads:
         copy.start()
@@ -347,9 +377,12 @@
     ]
     for flow in flows:
         flow.begin()
+    lane = lax.broadcasted_iota(jnp.int32, (1, V), 1)
+    line = jnp.zeros((1, V), f32)
+    for k in range(Q):
+        line = jnp.where(lane == k, dsm[k], line)
+    gd[place.z, place.y] = line
     Flow.relays(flows)
-    small = Flow(place, gd, slice(None), 1, (ad, bd))
-    small.begin()
     loads[3].wait()
     i = lax.broadcasted_iota(jnp.int32, (2 * V, 2 * V), 0)
     j = lax.broadcasted_iota(jnp.int32, (2 * V, 2 * V), 1)
@@ -361,7 +394,6 @@
         kown[1, :, tile * V : (tile + 1) * V] = moved[:, V:]
     swap = remote(kown.at[1 - place.core], kland, ksem.at[0], ksem.at[1], place.near(1)[2])
     swap.start()
-    Flow.relays([small])
     swap.wait()
     both = split(jnp.concatenate([kown[place.core], kland[...]], 0))
     rows = kland.shape[0]
@@ -371,6 +403,7 @@
     part[place.core] = image[:rows].reshape(nx, Q, 2 * V)
     part[1 - place.core] = image[rows:].reshape(nx, Q, 2 * V)
     scatter = Spread(place, lambda x, core: part.at[core, x], lambda i: landed.at[i], rs)
+    small = Lines(place, gd, ad, bd)
     sums = Sum(place, three(dot3(ys, ys, 0, 0)), m0, m1, m2, msem)
     scatter.arrive()
     total = part[place.core, place.x]
@@ -386,7 +419,10 @@
         flow.begin()
     sums.middle()
     Flow.relays(again)
-    small.end()
+    small.middle()
+    sums.arrive()
+    factor = metric_factor(rows_of(m2), work)
+    small.arrive()
     height = nz * ny * Q
     r = lax.broadcasted_iota(jnp.int32, (height, nz * ny), 0)
     b = lax.broadcasted_iota(jnp.int32, (height, nz * ny), 1)
@@ -395,24 +431,24 @@
     r = lax.broadcasted_iota(jnp.int32, (height, V), 0)
     b = lax.broadcasted_iota(jnp.int32, (height, V), 1)
     entry[...] = dot(jnp.where(r % Q == b, entries, 0.0), jnp.ones((V, V), f32))
-    sums.arrive()
-    factor = metric_factor(rows_of(m2), work)
     Flow.ends(again)
     zs = split(jnp.concatenate([rows_of(hx), rows_of(hw)], 1))
-    more = Sum(place, three(dot3(ys, zs, 0, 0)), p0, p1, p2, psem)
+    gram = three(dot3(ys, zs, 0, 0))
+    more = Sum(place, gram[: 2 * V], p0, p1, p2, psem)
+    rest = Sum(place, gram[2 * V :], r0, r1, r2, rsem)
     more.middle()
     more.arrive()
-    mix, ritz = first_mixing(factor, rows_of(p2), work)
+    mix, ritz = first_mixing(factor, rows_of(p2), rest, work)
     mixes = split(mix)
-    vectors, images = dot3(ys, mixes), dot3(zs, mixes)
-    vs = split(vectors)
-    search, squares = correction_of(images, vs, ritz, entry[...])
+    images = dot3(zs, mixes)
+    moved = dot3(ys, split(dot(mix, ritz)))
+    search, squares = correction_of(images, moved, ritz, entry[...])
     ws = split(search)
     image = dot3(both, ws)
     less[place.core] = image[:rows].reshape(nx, Q, V)
     less[1 - place.core] = image[rows:].reshape(nx, Q, V)
     rescatter = Spread(place, lambda x, core: less.at[core, x], lambda i: lessland.at[i], ts)
-    us = split(images)
+    vs, us = split(dot3(ys, mixes)), split(images)
     gram = jnp.concatenate([dot3(a, ws, 0, 0) for a in (vs, ws, us)], 0)
     cross = Sum(place, gram, q0, q1, q2, qsem)
     nsum[...] = jnp.broadcast_to(squares, (8, V))
@@ -449,13 +485,14 @@
     values = Sum(place, dot3(vs, split(images), 0, 0), l0, l1, l2, lsem)
     values.middle()
     values.arrive()
-    search, squares = correction_of(images, vs, rows_of(l2), entry[...])
+    ritz = rows_of(l2)
+    search, squares = correction_of(images, dot3(vs, split(ritz)), ritz, entry[...])
     osum[...] = jnp.broadcast_to(squares, (8, V))
     final = Spread(place, lambda x, core: osum, lambda i: oland.at[i], os)
     ss[...] = search
     search_out[...] = ss[own, :]
-    Flow.drain(flows + [small] + again + last)
-    for other in (scatter, sums, more, rescatter, cross, norms, values):
+    Flow.drain(flows + again + last)
+    for other in (small, scatter, sums, more, rest, rescatter, cross, norms, values):
         other.drain()
     final.arrive()
     squares = osum[...]
@@ -469,10 +506,10 @@
     nz, ny, _, nx = dims
     height, group, rows = nz * ny * Q, 2 * nx, nx * Q
     grid = pltpu.VMEM((nz, ny, Q, V), f32)
-    entries = jnp.pad(precond_diag, (0, V - Q)).reshape(1, V)
     small = [pltpu.VMEM((8, V), f32), pltpu.VMEM((group, 8, V), f32)]
     scratch = [grid] * 5 + [
         pltpu.VMEM((nz, ny, 1, V), f32),
+        pltpu.SMEM((Q,), f32),
         pltpu.VMEM((height, V), f32),
         pltpu.VMEM((rows, 2 * height), f32),
         pltpu.VMEM((2, rows, height), f32),
@@ -482,11 +519,13 @@
         pltpu.VMEM((2, nx, Q, V), f32),
         pltpu.VMEM((group, Q, V), f32),
     ]
-    scratch += sum_scratch(group, 3 * V // group) * 3 + sum_scratch(group, V // group)
+    for height_of in (3, 2, 1, 3, 1):
+        scratch += sum_scratch(group, height_of * V // group)
     scratch += small * 2 + [pltpu.VMEM((height, V), f32)] * 2 + [pltpu.VMEM((V, 2 * V), f32)]
     scratch += [pltpu.SemaphoreType.DMA((4,)), pltpu.SemaphoreType.DMA((2,))]
-    for _ in range(7):
+    for _ in range(6):
         scratch += flow_sems(dims)
+    scratch += [pltpu.SemaphoreType.DMA((nz + ny,))] * 2
     scratch += [near_sems() for _ in range(4)]
     return pl.pallas_call(
         functools.partial(davidson_kernel, dims),
@@ -495,7 +534,7 @@
         out_specs=(pl.BlockSpec(memory_space=pltpu.VMEM),) * 3,
         scratch_shapes=scratch,
         compiler_params=pltpu.CompilerParams(collective_id=0, has_side_effects=True),
-    )(kernel.reshape(rows, 2 * height), ritz_block, search_block, entries)
+    )(kernel, ritz_block, search_block, precond_diag)
 
 
 def solution(mesh):

time: 125 us -> 121 us (0.968)
  local copies, waits for them, and re-layouts: 5.69 us -> 2.5 us
    unnamed x8 -> x7, local copies, waits for them, and re-layouts: 4.52 us -> 2.5 us
where the time goes in v3:
time: 121 us
  Pallas kernels  118 us (98%)
  local copies, waits for them, and re-layouts  2.5 us (2%)
    pallas_call x1, Pallas kernels, per_device(): pl.pallas_call(functools.partial(davidson_kernel, dims), out_shape=tuple(...  118 us
    unnamed x7, local copies, waits for them, and re-layouts  2.5 us

profile of v3, /device:TPU:1, one launch (start us, length us, event | category | flops | bytes accessed | tf_op | source)
XLA Modules:
  0.0 120.7 jit_solution(1339117489580560744)
XLA Ops:
  0.6 117.6 %shard_map.67 = (f32[16,128]{1,0:T(8,128)}, f32[16,128]{1,0:T(8,128)}, f32[2,128]{1,0:T(2,128)}) custom-call(f32[64,1,2048]{2,1,0:T(1,128)} %k_in.1, f32[16,128]{1,0:T(8,128)} %x_in.1, f32[16,128]{1,0:T(8,128)} %w_in.1, f32[16]{0:T(128)} %d_in.1), custom_call_target="tpu_custom_call" | custom-call | tf_op jit(solution)/shard_map/pallas_call | solution.py:530
  118.2 0.0 copy-start
  118.2 1.3 %copy.10 = f32[16,128]{1,0:T(8,128)} copy(f32[16,128]{1,0:T(8,128)} %get-tuple-element.6) | data formatting | bytes 16384
  119.5 0.0 copy-done
  119.5 0.0 copy-start.1
  119.5 0.6 copy.11
  120.1 0.0 copy-done.1
  120.2 0.6 copy.12
Async XLA Ops:
  118.2 1.3 %copy-start = (f32[16,128]{1,0:T(8,128)S(1)}, f32[16,128]{1,0:T(8,128)}, u32[]{:S(2)}) copy-start(f32[16,128]{1,0:T(8,128)} %get-tuple-element.7) | copy-start | bytes 24580
  119.5 0.6 copy-start.1

commit v4 on v3

--- a/solution.py
+++ b/solution.py
@@ -240,7 +240,8 @@
     def __init__(self, place, source, target, sems):
         self.place = place
         self.copies = []
-        for i in range(1, 2 * place.dims[3]):
+        size = place.dims[3]
+        for i in sorted(range(1, 2 * size), key=lambda i: -min(i // 2, size - i // 2)):
             x, core, to = place.near(i)
             self.copies.append(
                 remote(source(x, core), target(i), sems.at[0, i], sems.at[1, i], to)
@@ -422,6 +423,11 @@
     small.middle()
     sums.arrive()
     factor = metric_factor(rows_of(m2), work)
+    Flow.ends(again)
+    zs = split(jnp.concatenate([rows_of(hx), rows_of(hw)], 1))
+    gram = three(dot3(ys, zs, 0, 0))
+    more = Sum(place, gram[: 2 * V], p0, p1, p2, psem)
+    rest = Sum(place, gram[2 * V :], r0, r1, r2, rsem)
     small.arrive()
     height = nz * ny * Q
     r = lax.broadcasted_iota(jnp.int32, (height, nz * ny), 0)
@@ -431,11 +437,6 @@
     r = lax.broadcasted_iota(jnp.int32, (height, V), 0)
     b = lax.broadcasted_iota(jnp.int32, (height, V), 1)
     entry[...] = dot(jnp.where(r % Q == b, entries, 0.0), jnp.ones((V, V), f32))
-    Flow.ends(again)
-    zs = split(jnp.concatenate([rows_of(hx), rows_of(hw)], 1))
-    gram = three(dot3(ys, zs, 0, 0))
-    more = Sum(place, gram[: 2 * V], p0, p1, p2, psem)
-    rest = Sum(place, gram[2 * V :], r0, r1, r2, rsem)
     more.middle()
     more.arrive()
     mix, ritz = first_mixing(factor, rows_of(p2), rest, work)

time: 121 us -> 117 us (0.967)
  Pallas kernels: 118 us -> 114 us
    pallas_call x1, Pallas kernels: 118 us -> 114 us  [per_device(): pl.pallas_call(functools.partial(davidson_kernel, dims), out_shape=tuple(...]
where the time goes in v4:
time: 117 us
  Pallas kernels  114 us (97%)
  local copies, waits for them, and re-layouts  2.5 us (2%)
    pallas_call x1, Pallas kernels, per_device(): pl.pallas_call(functools.partial(davidson_kernel, dims), out_shape=tuple(...  114 us
    unnamed x7, local copies, waits for them, and re-layouts  2.5 us

profile of v4, /device:TPU:1, one launch (start us, length us, event | category | flops | bytes accessed | tf_op | source)
XLA Modules:
  0.0 116.9 jit_solution(1766663997062214468)
XLA Ops:
  0.6 113.7 %shard_map.67 = (f32[16,128]{1,0:T(8,128)}, f32[16,128]{1,0:T(8,128)}, f32[2,128]{1,0:T(2,128)}) custom-call(f32[64,1,2048]{2,1,0:T(1,128)} %k_in.1, f32[16,128]{1,0:T(8,128)} %x_in.1, f32[16,128]{1,0:T(8,128)} %w_in.1, f32[16]{0:T(128)} %d_in.1), custom_call_target="tpu_custom_call" | custom-call | tf_op jit(solution)/shard_map/pallas_call | solution.py:531
  114.4 0.0 copy-start
  114.4 1.3 %copy.10 = f32[16,128]{1,0:T(8,128)} copy(f32[16,128]{1,0:T(8,128)} %get-tuple-element.6) | data formatting | bytes 16384
  115.7 0.0 copy-done
  115.7 0.0 copy-start.1
  115.7 0.6 copy.11
  116.3 0.0 copy-done.1
  116.3 0.6 copy.12
Async XLA Ops:
  114.4 1.3 %copy-start = (f32[16,128]{1,0:T(8,128)S(1)}, f32[16,128]{1,0:T(8,128)}, u32[]{:S(2)}) copy-start(f32[16,128]{1,0:T(8,128)} %get-tuple-element.7) | copy-start | bytes 24580
  115.7 0.6 copy-start.1
